TPU v7x, 32 devices: a whole 2x2x4 slice. The times are simulated.
32 devices in a mesh: kpt: 2 (over y), row: 8 (over z, x), freq: 2 (over core).
Axes of the slice: x: 2, y: 2, z: 4, core: 2. Of those that a mesh axis runs over, the one named last changes fastest.
Arguments:
- screened: bfloat16 [8, 2, 8192, 8192], P(('kpt', 'freq'), None, 'row'), parts along dimension 0, may hold values from -0.0625 to 0.0625
- elements: bfloat16 [2, 1024, 8192], P(None, 'kpt', 'row'), parts along dimension 1, may hold values from -0.59765625 to 0.59765625
- node_freq: float32 [4], P('freq'), may hold values from 0.1 to 2
- node_weight: float32 [4], P('freq'), may hold values from 0.1 to 1
- band_energy: float32 [1024], P('kpt'), parts along dimension 0, may hold values from -1 to 1
- energy_grid: float32 [64], replicated, may hold values from -1 to 1
- pair_state: int32 [1024], P('kpt'), parts along dimension 0, may hold values from 0 to 31
- pair_band: int32 [1024], P('kpt'), parts along dimension 0, may hold values from 0 to 511
Outputs:
- sigma: float32 [2, 64, 64], P(None, 'kpt'), parts along dimension 1
There are 2 independent parts, one for each index of `kpt`. A program takes and returns all parts, laid end to end along the dimension named above; an argument that names none is the same for every part. Nothing has to cross between parts.
All inputs are finite; a program needn't handle non-finite values.
Results may differ from a plain program's by a relative error of at most 0.0003.
Values may be sent and summed in bfloat16 or wider, within the bound.
A program may use at most 192 MiB of HBM per device.

v0:
```python
import jax
import jax.numpy as jnp
from jax import lax
from jax.sharding import PartitionSpec as P

NSTATE = 32


def product(weights, piece):
    return jnp.einsum("jgc,pc->jgp", weights, piece, preferred_element_type=jnp.float32)


def self_energy(
    form_re, form_im, node_freq, node_weight, band_energy, energy_grid, pair_state, pair_band
):
    band_onehot = (
        pair_band[:, None] == jnp.arange(band_energy.shape[0], dtype=jnp.int32)[None, :]
    ).astype(jnp.float32)
    pair_eps = jnp.dot(band_onehot, band_energy, precision=lax.Precision.HIGHEST)
    delta = energy_grid[None, :] - pair_eps[:, None]
    factor = (
        node_weight[:, None, None]
        * delta[None]
        / (delta[None] ** 2 + node_freq[:, None, None] ** 2)
    )
    terms_re = jnp.sum(form_re[:, :, None] * factor, axis=0)
    terms_im = jnp.sum(form_im[:, :, None] * factor, axis=0)
    state_onehot = (jnp.arange(NSTATE, dtype=jnp.int32)[:, None] == pair_state[None, :]).astype(
        jnp.float32
    )
    sig_re = jnp.dot(state_onehot, terms_re, precision=lax.Precision.HIGHEST)
    sig_im = jnp.dot(state_onehot, terms_im, precision=lax.Precision.HIGHEST)
    return jnp.stack([sig_re, sig_im])


def per_device(
    screened, elements, node_freq, node_weight, band_energy, energy_grid, pair_state, pair_band
):
    w_real = screened[:, 0]
    w_imag = screened[:, 1]
    npair = elements.shape[1]
    half = npair // lax.axis_size("freq")
    mine = lax.dynamic_slice_in_dim(elements, lax.axis_index("freq") * half, half, 1)
    collected = lax.all_gather(mine, "row", axis=2, tiled=True)
    piece = lax.all_gather(collected, "freq", axis=1, tiled=True)
    part_real = product(w_real, piece[0]) - product(w_imag, piece[1])
    part_imag = product(w_real, piece[1]) + product(w_imag, piece[0])
    stacked = jnp.stack([part_real, part_imag])
    y_real = stacked[0]
    y_imag = stacked[1]
    own_real = elements[0].T.astype(jnp.float32)[None]
    own_imag = elements[1].T.astype(jnp.float32)[None]
    form_re = jnp.sum(own_real * y_real + own_imag * y_imag, axis=1)
    form_im = jnp.sum(own_real * y_imag - own_imag * y_real, axis=1)
    form_re, form_im = lax.psum((form_re, form_im), "row")
    partial_sigma = self_energy(
        form_re, form_im, node_freq, node_weight, band_energy, energy_grid, pair_state, pair_band
    )
    return lax.psum(partial_sigma, "freq")


def solution(mesh):
    in_specs = (
        P(("kpt", "freq"), None, "row", None),
        P(None, "kpt", "row"),
        P("freq"),
        P("freq"),
        P("kpt"),
        P(),
        P("kpt"),
        P("kpt"),
    )
    out_specs = P(None, "kpt", None)
    return jax.shard_map(
        per_device, mesh=mesh, in_specs=in_specs, out_specs=out_specs, check_vma=False
    )
```

profile of v0, /device:TPU:0, one launch (start us, length us, event | category | flops | bytes accessed | tf_op | source)
XLA Modules:
  0.0 302.2 jit_solution(1204558639361420559)
XLA Ops:
  6.5 0.0 copy-start
  6.5 0.0 copy-start.1
  6.5 0.0 copy-start.10
  6.5 0.0 copy-start.9
  6.5 0.0 copy-start.6
  6.5 0.0 all-gather.3.cloned.1.call-start
  6.6 2.4 constant_dynamic-slice_fusion
  9.0 0.0 all-gather.3.cloned.1.call-update
  9.0 0.0 all-gather.5.cloned.1.call-start
  9.1 127.7 %all-gather.3.cloned.1.call-done = bf16[2,256,8192]{2,1,0:T(8,128)(2,1)} async-done(((bf16[2,256,1024]{2,1,0:T(8,128)(2,1)}), bf16[2,256,8192]{2,1,0:T(8,128)(2,1)}) %all-gather.3.cloned.1.call-update) | async-done | bytes 8388624 | tf_op jit(solution)/shard_map/all_gather | solution.py:44
  136.8 0.0 all-gather.5.cloned.1.call-update
  136.8 0.0 copy-done.10
  136.8 0.5 integer_pow.13
  137.3 0.0 copy-done
  137.3 0.0 copy-done.9
  137.3 0.6 fusion.16
  137.9 0.0 copy-done.6
  137.9 0.8 broadcast_subtract_fusion
  138.7 0.0 copy-done.1
  138.7 2.5 convert_bitcast_fusion.1
  141.2 25.4 %all-gather.5.cloned.1.call-done = bf16[2,512,8192]{2,1,0:T(8,128)(2,1)} async-done(((bf16[2,256,8192]{2,1,0:T(8,128)(2,1)}), bf16[2,512,8192]{2,1,0:T(8,128)(2,1)}) %all-gather.5.cloned.1.call-update) | async-done | bytes 16777232 | tf_op jit(solution)/shard_map/all_gather | solution.py:45
  166.6 24.9 %fusion = f32[512,2,1024]{2,0,1:T(8,128)} fusion(bf16[2,2,1024,8192]{3,2,1,0:T(8,128)(2,1)} %param.8, bf16[2,512,8192]{2,1,0:T(8,128)(2,1)} %all-gather.5.cloned.1.call-done), kind=kOutput, calls=%fused_computation | convolution fusion | flops 17179869184 | bytes 46137344 | tf_op jit(solution)/shard_map/jgc,pc->jgp/dot_general | solution.py:10
  191.5 24.9 %fusion.2 = f32[512,2,1024]{2,0,1:T(8,128)} fusion(bf16[2,2,1024,8192]{3,2,1,0:T(8,128)(2,1)} %param.8, bf16[2,512,8192]{2,1,0:T(8,128)(2,1)} %all-gather.5.cloned.1.call-done), kind=kOutput, calls=%fused_computation.2 | convolution fusion | flops 17179869184 | bytes 46137344 | tf_op jit(solution)/shard_map/jgc,pc->jgp/dot_general | solution.py:10
  216.5 0.0 copy-start.2
  216.5 25.1 %fusion.6 = f32[512,2,1024]{2,0,1:T(8,128)} fusion(bf16[2,2,1024,8192]{3,2,1,0:T(8,128)(2,1)} %param.8, bf16[2,512,8192]{2,1,0:T(8,128)(2,1)} %all-gather.5.cloned.1.call-done), kind=kOutput, calls=%fused_computation.6 | convolution fusion | flops 17179869184 | bytes 46137344 | tf_op jit(solution)/shard_map/jgc,pc->jgp/dot_general | solution.py:10
  241.5 0.0 copy-done.2
  241.5 0.0 copy-start.3
  241.6 0.0 copy-start.4
  241.6 0.0 copy-start.7
  241.6 0.0 copy-start.8
  241.6 0.0 copy-start.5
  241.6 27.3 %fusion.13 = (f32[2,512]{1,0:T(2,128)S(1)}, f32[2,512]{1,0:T(2,128)S(1)}) fusion(f32[1024,512]{0,1:T(8,128)} %get-tuple-element.12, f32[1024,512]{0,1:T(8,128)S(1)} %copy-done.2, f32[512,2,1024]{2,0,1:T(8,128)} %fusion, f32[512,2,1024]{2,0,1:T(8,128)} %fusion.6, f32[512,2,1024]{2,0,1:T(8,128)} %fusion.2, bf16[2,2,1024,8192]{3,2,1,0:T(8,128)(2,1)} %param.8, ...), kind=kOutput, calls=%fused_computation.17 | convolution fusion | flops 17190354944 | bytes 58728448 | tf_op jit(solution)/shard_map/jgc,pc->jgp/dot_general | solution.py:10
  268.9 21.9 %all-reduce = (f32[2,512]{1,0:T(2,128)S(1)}, f32[2,512]{1,0:T(2,128)S(1)}) all-reduce(f32[2,512]{1,0:T(2,128)S(1)} %get-tuple-element.5, f32[2,512]{1,0:T(2,128)S(1)} %get-tuple-element.6), channel_id=1, replica_groups=mesh['kpt'=2,'row'=8,'freq'=2] {'row'}, use_global_device_ids=true, to_apply=%region_1.0 | all-reduce | flops 2048 | bytes 16384 | tf_op jit(solution)/shard_map/psum | solution.py:55
  290.8 0.0 copy-done.3
  290.8 0.0 copy-done.4
  290.8 0.0 copy-done.7
  290.8 0.0 copy-done.8
  290.8 0.1 multiply_reduce_fusion.1
  291.0 0.0 copy-done.5
  291.0 0.2 convolution_bitcast_fusion
  291.2 0.2 convolution_bitcast_fusion.1
  291.4 4.0 %psum.23 = f32[2,32,64]{2,1,0:T(8,128)} all-reduce(f32[2,32,64]{2,1,0:T(8,128)S(1)} %pad_maximum_fusion), channel_id=1, replica_groups=mesh['kpt'=2,'row'=8,'freq'=2] {'freq'}, use_global_device_ids=true, to_apply=%region_6.0 | all-reduce | flops 4096 | bytes 32768 | tf_op jit(solution)/shard_map/psum | solution.py:59
  (1 shorter events, 0.0 us)
Async XLA Ops:
  6.5 130.8 %copy-start = (f32[512]{0:T(512)S(1)}, f32[512]{0:T(512)}, u32[]{:S(2)}) copy-start(f32[512]{0:T(512)} %param.12) | copy-start | bytes 6148
  6.5 132.2 %copy-start.1 = (bf16[2,512,1024]{2,1,0:T(8,128)(2,1)S(1)}, bf16[2,512,1024]{2,1,0:T(8,128)(2,1)}, u32[]{:S(2)}) copy-start(bf16[2,512,1024]{2,1,0:T(8,128)(2,1)} %param.9) | copy-start | bytes 6291460
  6.5 130.2 %copy-start.10 = (f32[2]{0:T(128)S(1)}, f32[2]{0:T(128)}, u32[]{:S(2)}) copy-start(f32[2]{0:T(128)} %param.10) | copy-start | bytes 28
  6.5 130.8 %copy-start.9 = (s32[512]{0:T(512)S(1)}, s32[512]{0:T(512)}, u32[]{:S(2)}) copy-start(s32[512]{0:T(512)} %param.15) | copy-start | bytes 6148
  6.5 131.4 %copy-start.6 = (f32[64]{0:T(128)S(1)}, f32[64]{0:T(128)}, u32[]{:S(2)}) copy-start(f32[64]{0:T(128)} %param.13) | copy-start | bytes 772
  6.5 130.2 %all-gather.3.cloned.1.call-start = ((), (), s32[]{:S(2)}) async-start(), calls=%async_computation | async-start | bytes 9437184 | tf_op jit(solution)/shard_map/all_gather | solution.py:44
  9.0 157.6 %all-gather.5.cloned.1.call-start = ((), (), s32[]{:S(2)}) async-start(), calls=%async_computation.1 | async-start | bytes 25165824 | tf_op jit(solution)/shard_map/all_gather | solution.py:45
  216.5 25.1 %copy-start.2 = (f32[1024,512]{0,1:T(8,128)S(1)}, f32[1024,512]{0,1:T(8,128)}, u32[]{:S(2)}) copy-start(f32[1024,512]{0,1:T(8,128)} %get-tuple-element.11) | copy-start | bytes 6291460
  241.5 49.2 %copy-start.3 = (f32[512,64]{0,1:T(8,128)S(1)}, f32[512,64]{0,1:T(8,128)}, u32[]{:S(2)}) copy-start(f32[512,64]{0,1:T(8,128)} %get-tuple-element.13) | copy-start | bytes 393220
  241.6 49.2 %copy-start.4 = (f32[512,64]{0,1:T(8,128)S(1)}, f32[512,64]{0,1:T(8,128)}, u32[]{:S(2)}) copy-start(f32[512,64]{0,1:T(8,128)} %get-tuple-element.14) | copy-start | bytes 393220
  241.6 49.3 %copy-start.7 = (f32[2]{0:T(128)S(1)}, f32[2]{0:T(128)}, u32[]{:S(2)}) copy-start(f32[2]{0:T(128)} %param.11) | copy-start | bytes 28
  241.6 49.3 %copy-start.8 = (f32[2]{0:T(128)S(1)}, f32[2]{0:T(128)}, u32[]{:S(2)}) copy-start(f32[2]{0:T(128)} %integer_pow.13) | copy-start | bytes 28
  241.6 49.4 %copy-start.5 = (s32[512]{0:T(512)S(1)}, s32[512]{0:T(512)}, u32[]{:S(2)}) copy-start(s32[512]{0:T(512)} %param.14) | copy-start | bytes 6148
Sparse Core Ops, SparseCore 0:
  9.5 127.1 all-gather.2
  138.3 28.2 all-gather.4
where the time goes:
time: 302 us
  waiting for transfers between devices  153 us (51%)
  matrix products  103 us (34%)
  blocking collectives  25.9 us (9%)
  between operations  13.5 us (4%)
  other arithmetic  3.93 us (1%)
    all_gather x1, waiting for transfers between devices, per_device(): collected = lax.all_gather(mine, 'row', axis=2, tiled=True)  128 us
    dot_general x4, matrix products, product(): jnp.einsum('jgc,pc->jgp', weights, piece, preferred_element_type=jnp.floa...  102 us
    all_gather x1, waiting for transfers between devices, per_device(): piece = lax.all_gather(collected, 'freq', axis=1, tiled=True)  25.4 us
    psum x1, blocking collectives, per_device(): form_re, form_im = lax.psum((form_re, form_im), 'row')  21.9 us
  transfers between devices with their start and end apart: 2, of which 2 were waited for; matrix products, arithmetic and copies ran while one was open for 1% of the time, Pallas kernels for 0%

commit v1 on v0

--- a/solution.py
+++ b/solution.py
@@ -41,7 +41,12 @@
     npair = elements.shape[1]
     half = npair // lax.axis_size("freq")
     mine = lax.dynamic_slice_in_dim(elements, lax.axis_index("freq") * half, half, 1)
-    collected = lax.all_gather(mine, "row", axis=2, tiled=True)
+    ring = [mine]
+    for hop in range(7):
+        ring.append(lax.ppermute(ring[-1], "row", [(dev, (dev + 1) % 8) for dev in range(8)]))
+    collected = jnp.roll(
+        jnp.concatenate(ring[::-1], axis=2), (lax.axis_index("row") + 1) * ring[0].shape[2], axis=2
+    )
     piece = lax.all_gather(collected, "freq", axis=1, tiled=True)
     part_real = product(w_real, piece[0]) - product(w_imag, piece[1])
     part_imag = product(w_real, piece[1]) + product(w_imag, piece[0])

time: 302 us -> 388 us (1.28)
  waiting for transfers between devices: 153 us -> 197 us
  local copies, waits for them, and re-layouts: 2.45 us -> 39.7 us
    ppermute x0 -> x7, waiting for transfers between devices: none -> 176 us  [per_device(): lax.ppermute(ring[-1], 'row', [(dev, (dev + 1) % 8) for dev in range(8)])]
    all_gather x1 -> x0, waiting for transfers between devices: 128 us -> none  [per_device(): collected = lax.all_gather(mine, 'row', axis=2, tiled=True)]
    unnamed x22 -> x55, local copies, waits for them, and re-layouts: 0.05 us -> 29.6 us
    dynamic_slice x0 -> x1, local copies, waits for them, and re-layouts: none -> 7.6 us  [per_device(): jnp.roll(jnp.concatenate(ring[::-1], axis=2), (lax.axis_index('row') + 1)...]
    all_gather x1, waiting for transfers between devices: 25.4 us -> 21.3 us  [per_device(): piece = lax.all_gather(collected, 'freq', axis=1, tiled=True)]
  transfers between devices with their start and end apart: 2 -> 8, of which waited for: 2 -> 8; matrix products, arithmetic and copies ran while one was open for 1% -> 1% of each run, Pallas kernels for 0% -> 0%
where the time goes in v1:
time: 388 us; the launch traced here: 387 us
  waiting for transfers between devices  197 us (51%)
  matrix products  103 us (27%)
  local copies, waits for them, and re-layouts  39.7 us (10%)
  blocking collectives  25.9 us (7%)
  between operations  13.6 us (4%)
  other arithmetic  4.57 us (1%)
    ppermute x7, waiting for transfers between devices, per_device(): lax.ppermute(ring[-1], 'row', [(dev, (dev + 1) % 8) for dev in range(8)])  176 us
    dot_general x4, matrix products, product(): jnp.einsum('jgc,pc->jgp', weights, piece, preferred_element_type=jnp.floa...  102 us
    unnamed x55, local copies, waits for them, and re-layouts  29.6 us
    psum x1, blocking collectives, per_device(): form_re, form_im = lax.psum((form_re, form_im), 'row')  21.9 us
    all_gather x1, waiting for transfers between devices, per_device(): piece = lax.all_gather(collected, 'freq', axis=1, tiled=True)  21.3 us
  transfers between devices with their start and end apart: 8, of which 8 were waited for; matrix products, arithmetic and copies ran while one was open for 1% of the time, Pallas kernels for 0%

profile of v1, /device:TPU:0, one launch (start us, length us, event | category | flops | bytes accessed | tf_op | source)
XLA Modules:
  0.0 387.2 jit_solution(2989809023601234066)
XLA Ops:
  6.5 0.0 copy-start
  6.5 0.0 all-gather.2.cloned.1.call-start
  6.5 1.4 constant_dynamic-slice_fusion.1
  8.0 3.0 collective-permute-start
  11.0 26.2 %collective-permute-done = bf16[2,256,1024]{2,1,0:T(8,128)(2,1)S(1)} collective-permute-done((bf16[2,256,1024]{2,1,0:T(8,128)(2,1)S(1)}, bf16[2,256,1024]{2,1,0:T(8,128)(2,1)S(1)}, u32[]{:S(2)}, u32[]{:S(2)}) %collective-permute-start) | collective-permute-done | bytes 1048608 | tf_op jit(solution)/shard_map/ppermute | solution.py:46
  37.2 0.0 collective-permute-start.1
  37.2 27.0 %collective-permute-done.1 = bf16[2,256,1024]{2,1,0:T(8,128)(2,1)S(1)} collective-permute-done((bf16[2,256,1024]{2,1,0:T(8,128)(2,1)S(1)}, bf16[2,256,1024]{2,1,0:T(8,128)(2,1)S(1)}, u32[]{:S(2)}, u32[]{:S(2)}) %collective-permute-start.1) | collective-permute-done | bytes 1048608 | tf_op jit(solution)/shard_map/ppermute | solution.py:46
  64.2 1.0 copy-done.3
  65.2 0.0 collective-permute-start.2
  65.2 26.2 %collective-permute-done.2 = bf16[2,256,1024]{2,1,0:T(8,128)(2,1)S(1)} collective-permute-done((bf16[2,256,1024]{2,1,0:T(8,128)(2,1)S(1)}, bf16[2,256,1024]{2,1,0:T(8,128)(2,1)S(1)}, u32[]{:S(2)}, u32[]{:S(2)}) %collective-permute-start.2) | collective-permute-done | bytes 1048608 | tf_op jit(solution)/shard_map/ppermute | solution.py:46
  91.4 1.0 copy-done.5
  92.4 0.0 collective-permute-start.3
  92.4 25.3 %collective-permute-done.3 = bf16[2,256,1024]{2,1,0:T(8,128)(2,1)S(1)} collective-permute-done((bf16[2,256,1024]{2,1,0:T(8,128)(2,1)S(1)}, bf16[2,256,1024]{2,1,0:T(8,128)(2,1)S(1)}, u32[]{:S(2)}, u32[]{:S(2)}) %collective-permute-start.3) | collective-permute-done | bytes 1048608 | tf_op jit(solution)/shard_map/ppermute | solution.py:46
  117.7 1.0 copy-done.7
  118.7 0.0 collective-permute-start.4
  118.7 24.4 %collective-permute-done.4 = bf16[2,256,1024]{2,1,0:T(8,128)(2,1)S(1)} collective-permute-done((bf16[2,256,1024]{2,1,0:T(8,128)(2,1)S(1)}, bf16[2,256,1024]{2,1,0:T(8,128)(2,1)S(1)}, u32[]{:S(2)}, u32[]{:S(2)}) %collective-permute-start.4) | collective-permute-done | bytes 1048608 | tf_op jit(solution)/shard_map/ppermute | solution.py:46
  143.1 1.0 copy-done.9
  144.1 0.0 collective-permute-start.5
  144.1 23.7 %collective-permute-done.5 = bf16[2,256,1024]{2,1,0:T(8,128)(2,1)} collective-permute-done((bf16[2,256,1024]{2,1,0:T(8,128)(2,1)S(1)}, bf16[2,256,1024]{2,1,0:T(8,128)(2,1)}, u32[]{:S(2)}, u32[]{:S(2)}) %collective-permute-start.5) | collective-permute-done | bytes 1048608 | tf_op jit(solution)/shard_map/ppermute | solution.py:46
  167.8 0.0 collective-permute-start.6
  167.8 0.0 copy-start.4
  167.9 23.0 %collective-permute-done.6 = bf16[2,256,1024]{2,1,0:T(8,128)(2,1)} collective-permute-done((bf16[2,256,1024]{2,1,0:T(8,128)(2,1)}, bf16[2,256,1024]{2,1,0:T(8,128)(2,1)}, u32[]{:S(2)}, u32[]{:S(2)}) %collective-permute-start.6) | collective-permute-done | bytes 1048608 | tf_op jit(solution)/shard_map/ppermute | solution.py:46
  190.9 2.3 constant_dynamic-update-slice_fusion.15
  193.2 2.3 constant_dynamic-update-slice_fusion.14
  195.5 2.2 constant_dynamic-update-slice_fusion.13
  197.7 2.3 constant_dynamic-update-slice_fusion.12
  200.0 2.3 constant_dynamic-update-slice_fusion.11
  202.3 2.3 constant_dynamic-update-slice_fusion.10
  204.6 1.0 constant_dynamic-update-slice_fusion.9
  205.6 0.0 copy-done.2
  205.6 1.0 constant_dynamic-update-slice_fusion.8
  206.7 2.3 constant_dynamic-update-slice_fusion.7
  208.9 2.3 constant_dynamic-update-slice_fusion.6
  211.2 0.0 copy-done.10
  211.2 1.0 constant_dynamic-update-slice_fusion.5
  212.2 0.0 copy-done.8
  212.2 1.0 constant_dynamic-update-slice_fusion.4
  213.3 0.0 copy-done.6
  213.3 1.1 constant_dynamic-update-slice_fusion.3
  214.4 0.0 copy-done.4
  214.4 1.1 constant_dynamic-update-slice_fusion.2
  215.4 1.1 constant_dynamic-update-slice_fusion.1
  216.5 1.1 constant_dynamic-update-slice_fusion
  217.6 7.6 %constant_dynamic-slice_fusion = bf16[2,256,8192]{2,1,0:T(8,128)(2,1)} fusion(bf16[2,256,16384]{2,1,0:T(8,128)(2,1)} %constant_dynamic-update-slice_fusion, s32[]{:T(128)S(6)} %select_n.18), kind=kLoop, calls=%fused_computation.54 | loop fusion | bytes 16777220 | tf_op jit(solution)/shard_map/jit(_roll_dynamic)/dynamic_slice | solution.py:47
  225.2 0.0 all-gather.2.cloned.1.call-update
  225.2 0.5 integer_pow.13
  225.7 0.0 copy-done.18
  225.7 0.6 fusion.16
  226.3 0.8 broadcast_subtract_fusion
  227.1 3.1 convert_bitcast_fusion.1
  230.3 21.3 %all-gather.2.cloned.1.call-done = bf16[2,512,8192]{2,1,0:T(8,128)(2,1)} async-done(((bf16[2,256,8192]{2,1,0:T(8,128)(2,1)}), bf16[2,512,8192]{2,1,0:T(8,128)(2,1)}) %all-gather.2.cloned.1.call-update) | async-done | bytes 16777232 | tf_op jit(solution)/shard_map/all_gather | solution.py:50
  251.5 24.9 %fusion = f32[512,2,1024]{2,0,1:T(8,128)} fusion(bf16[2,2,1024,8192]{3,2,1,0:T(8,128)(2,1)} %param.8, bf16[2,512,8192]{2,1,0:T(8,128)(2,1)} %all-gather.2.cloned.1.call-done), kind=kOutput, calls=%fused_computation | convolution fusion | flops 17179869184 | bytes 46137344 | tf_op jit(solution)/shard_map/jgc,pc->jgp/dot_general | solution.py:10
  276.5 24.9 %fusion.2 = f32[512,2,1024]{2,0,1:T(8,128)} fusion(bf16[2,2,1024,8192]{3,2,1,0:T(8,128)(2,1)} %param.8, bf16[2,512,8192]{2,1,0:T(8,128)(2,1)} %all-gather.2.cloned.1.call-done), kind=kOutput, calls=%fused_computation.2 | convolution fusion | flops 17179869184 | bytes 46137344 | tf_op jit(solution)/shard_map/jgc,pc->jgp/dot_general | solution.py:10
  301.4 25.1 %fusion.6 = f32[512,2,1024]{2,0,1:T(8,128)} fusion(bf16[2,2,1024,8192]{3,2,1,0:T(8,128)(2,1)} %param.8, bf16[2,512,8192]{2,1,0:T(8,128)(2,1)} %all-gather.2.cloned.1.call-done), kind=kOutput, calls=%fused_computation.6 | convolution fusion | flops 17179869184 | bytes 46137344 | tf_op jit(solution)/shard_map/jgc,pc->jgp/dot_general | solution.py:10
  326.5 0.0 copy-start.16
  326.5 0.0 copy-start.17
  326.5 0.0 copy-start.14
  326.5 0.0 copy-start.1
  326.5 27.3 %fusion.13 = (f32[2,512]{1,0:T(2,128)S(1)}, f32[2,512]{1,0:T(2,128)S(1)}) fusion(f32[1024,512]{0,1:T(8,128)} %get-tuple-element.12, f32[1024,512]{0,1:T(8,128)S(1)} %copy-done.11, f32[512,2,1024]{2,0,1:T(8,128)} %fusion, f32[512,2,1024]{2,0,1:T(8,128)} %fusion.6, f32[512,2,1024]{2,0,1:T(8,128)} %fusion.2, bf16[2,2,1024,8192]{3,2,1,0:T(8,128)(2,1)} %param.8, ...), kind=kOutput, calls=%fused_computation.17 | convolution fusion | flops 17190354944 | bytes 58728448 | tf_op jit(solution)/shard_map/jgc,pc->jgp/dot_general | solution.py:10
  353.9 21.9 %all-reduce = (f32[2,512]{1,0:T(2,128)S(1)}, f32[2,512]{1,0:T(2,128)S(1)}) all-reduce(f32[2,512]{1,0:T(2,128)S(1)} %get-tuple-element.5, f32[2,512]{1,0:T(2,128)S(1)} %get-tuple-element.6), channel_id=1, replica_groups=mesh['kpt'=2,'row'=8,'freq'=2] {'row'}, use_global_device_ids=true, to_apply=%region_1.2 | all-reduce | flops 2048 | bytes 16384 | tf_op jit(solution)/shard_map/psum | solution.py:60
  375.8 0.1 multiply_reduce_fusion.1
  376.0 0.2 convolution_bitcast_fusion
  376.2 0.2 convolution_bitcast_fusion.1
  376.4 4.0 %psum.23 = f32[2,32,64]{2,1,0:T(8,128)} all-reduce(f32[2,32,64]{2,1,0:T(8,128)S(1)} %pad_maximum_fusion), channel_id=1, replica_groups=mesh['kpt'=2,'row'=8,'freq'=2] {'freq'}, use_global_device_ids=true, to_apply=%region_6.7 | all-reduce | flops 4096 | bytes 32768 | tf_op jit(solution)/shard_map/psum | solution.py:64
  (25 shorter events, 0.0 us)
Async XLA Ops:
  6.5 219.2 %copy-start = (f32[512]{0:T(512)S(1)}, f32[512]{0:T(512)}, u32[]{:S(2)}) copy-start(f32[512]{0:T(512)} %param.12) | copy-start | bytes 6148
  6.5 199.1 %copy-start.2 = (bf16[2,512,1024]{2,1,0:T(8,128)(2,1)S(1)}, bf16[2,512,1024]{2,1,0:T(8,128)(2,1)}, u32[]{:S(2)}) copy-start(bf16[2,512,1024]{2,1,0:T(8,128)(2,1)} %param.9) | copy-start | bytes 6291460
  6.5 245.0 %all-gather.2.cloned.1.call-start = ((), (), s32[]{:S(2)}) async-start(), calls=%async_computation | async-start | bytes 25165824 | tf_op jit(solution)/shard_map/all_gather | solution.py:50
  8.0 29.2 %collective-permute-start = (bf16[2,256,1024]{2,1,0:T(8,128)(2,1)S(1)}, bf16[2,256,1024]{2,1,0:T(8,128)(2,1)S(1)}, u32[]{:S(2)}, u32[]{:S(2)}) collective-permute-start(bf16[2,256,1024]{2,1,0:T(8,128)(2,1)S(1)} %constant_dynamic-slice_fusion.1), channel_id=1, source_target_pairs={{0,2},{2,4},{4,6},{6,8},{8,10},{10,12},{12,14},{14,0},{1,3},{3,5},... | collective-permute-start | bytes 3145736 | tf_op jit(solution)/shard_map/ppermute | solution.py:46
  37.2 27.0 %collective-permute-start.1 = (bf16[2,256,1024]{2,1,0:T(8,128)(2,1)S(1)}, bf16[2,256,1024]{2,1,0:T(8,128)(2,1)S(1)}, u32[]{:S(2)}, u32[]{:S(2)}) collective-permute-start(bf16[2,256,1024]{2,1,0:T(8,128)(2,1)S(1)} %collective-permute-done), channel_id=1, source_target_pairs={{0,2},{2,4},{4,6},{6,8},{8,10},{10,12},{12,14},{14,0},{1,3},{3,5},... | collective-permute-start | bytes 3145736 | tf_op jit(solution)/shard_map/ppermute | solution.py:46
  64.2 1.0 copy-start.3
  65.2 26.2 %collective-permute-start.2 = (bf16[2,256,1024]{2,1,0:T(8,128)(2,1)S(1)}, bf16[2,256,1024]{2,1,0:T(8,128)(2,1)S(1)}, u32[]{:S(2)}, u32[]{:S(2)}) collective-permute-start(bf16[2,256,1024]{2,1,0:T(8,128)(2,1)S(1)} %collective-permute-done.1), channel_id=1, source_target_pairs={{0,2},{2,4},{4,6},{6,8},{8,10},{10,12},{12,14},{14,0},{1,3},{3,5},... | collective-permute-start | bytes 3145736 | tf_op jit(solution)/shard_map/ppermute | solution.py:46
  91.4 1.0 copy-start.5
  92.4 25.3 %collective-permute-start.3 = (bf16[2,256,1024]{2,1,0:T(8,128)(2,1)S(1)}, bf16[2,256,1024]{2,1,0:T(8,128)(2,1)S(1)}, u32[]{:S(2)}, u32[]{:S(2)}) collective-permute-start(bf16[2,256,1024]{2,1,0:T(8,128)(2,1)S(1)} %collective-permute-done.2), channel_id=1, source_target_pairs={{0,2},{2,4},{4,6},{6,8},{8,10},{10,12},{12,14},{14,0},{1,3},{3,5},... | collective-permute-start | bytes 3145736 | tf_op jit(solution)/shard_map/ppermute | solution.py:46
  117.7 1.0 copy-start.7
  118.7 24.5 %collective-permute-start.4 = (bf16[2,256,1024]{2,1,0:T(8,128)(2,1)S(1)}, bf16[2,256,1024]{2,1,0:T(8,128)(2,1)S(1)}, u32[]{:S(2)}, u32[]{:S(2)}) collective-permute-start(bf16[2,256,1024]{2,1,0:T(8,128)(2,1)S(1)} %collective-permute-done.3), channel_id=1, source_target_pairs={{0,2},{2,4},{4,6},{6,8},{8,10},{10,12},{12,14},{14,0},{1,3},{3,5},... | collective-permute-start | bytes 3145736 | tf_op jit(solution)/shard_map/ppermute | solution.py:46
  143.1 1.0 copy-start.9
  144.1 23.7 %collective-permute-start.5 = (bf16[2,256,1024]{2,1,0:T(8,128)(2,1)S(1)}, bf16[2,256,1024]{2,1,0:T(8,128)(2,1)}, u32[]{:S(2)}, u32[]{:S(2)}) collective-permute-start(bf16[2,256,1024]{2,1,0:T(8,128)(2,1)S(1)} %collective-permute-done.4), channel_id=1, source_target_pairs={{0,2},{2,4},{4,6},{6,8},{8,10},{10,12},{12,14},{14,0},{1,3},{3,5},... | collective-permute-start | bytes 3145736 | tf_op jit(solution)/shard_map/ppermute | solution.py:46
  167.8 23.1 %collective-permute-start.6 = (bf16[2,256,1024]{2,1,0:T(8,128)(2,1)}, bf16[2,256,1024]{2,1,0:T(8,128)(2,1)}, u32[]{:S(2)}, u32[]{:S(2)}) collective-permute-start(bf16[2,256,1024]{2,1,0:T(8,128)(2,1)} %collective-permute-done.5), channel_id=1, source_target_pairs={{0,2},{2,4},{4,6},{6,8},{8,10},{10,12},{12,14},{14,0},{1,3},{3,5},... | collective-permute-start | bytes 3145736 | tf_op jit(solution)/shard_map/ppermute | solution.py:46
  167.8 43.4 %copy-start.10 = (bf16[2,256,1024]{2,1,0:T(8,128)(2,1)S(1)}, bf16[2,256,1024]{2,1,0:T(8,128)(2,1)}, u32[]{:S(2)}) copy-start(bf16[2,256,1024]{2,1,0:T(8,128)(2,1)} %copy-done.9) | copy-start | bytes 3145732
  167.8 44.4 %copy-start.8 = (bf16[2,256,1024]{2,1,0:T(8,128)(2,1)S(1)}, bf16[2,256,1024]{2,1,0:T(8,128)(2,1)}, u32[]{:S(2)}) copy-start(bf16[2,256,1024]{2,1,0:T(8,128)(2,1)} %copy-done.7) | copy-start | bytes 3145732
  167.8 45.4 %copy-start.6 = (bf16[2,256,1024]{2,1,0:T(8,128)(2,1)S(1)}, bf16[2,256,1024]{2,1,0:T(8,128)(2,1)}, u32[]{:S(2)}) copy-start(bf16[2,256,1024]{2,1,0:T(8,128)(2,1)} %copy-done.5) | copy-start | bytes 3145732
  167.8 46.5 %copy-start.4 = (bf16[2,256,1024]{2,1,0:T(8,128)(2,1)S(1)}, bf16[2,256,1024]{2,1,0:T(8,128)(2,1)}, u32[]{:S(2)}) copy-start(bf16[2,256,1024]{2,1,0:T(8,128)(2,1)} %copy-done.3) | copy-start | bytes 3145732
  213.3 11.9 %copy-start.19 = (f32[2]{0:T(128)S(1)}, f32[2]{0:T(128)}, u32[]{:S(2)}) copy-start(f32[2]{0:T(128)} %param.10) | copy-start | bytes 28
  213.3 12.4 %copy-start.18 = (s32[512]{0:T(512)S(1)}, s32[512]{0:T(512)}, u32[]{:S(2)}) copy-start(s32[512]{0:T(512)} %param.15) | copy-start | bytes 6148
  213.3 13.1 %copy-start.15 = (f32[64]{0:T(128)S(1)}, f32[64]{0:T(128)}, u32[]{:S(2)}) copy-start(f32[64]{0:T(128)} %param.13) | copy-start | bytes 772
  301.4 25.1 %copy-start.11 = (f32[1024,512]{0,1:T(8,128)S(1)}, f32[1024,512]{0,1:T(8,128)}, u32[]{:S(2)}) copy-start(f32[1024,512]{0,1:T(8,128)} %get-tuple-element.11) | copy-start | bytes 6291460
  326.5 49.3 %copy-start.12 = (f32[512,64]{0,1:T(8,128)S(1)}, f32[512,64]{0,1:T(8,128)}, u32[]{:S(2)}) copy-start(f32[512,64]{0,1:T(8,128)} %get-tuple-element.13) | copy-start | bytes 393220
  326.5 49.3 %copy-start.13 = (f32[512,64]{0,1:T(8,128)S(1)}, f32[512,64]{0,1:T(8,128)}, u32[]{:S(2)}) copy-start(f32[512,64]{0,1:T(8,128)} %get-tuple-element.14) | copy-start | bytes 393220
  326.5 49.3 %copy-start.16 = (f32[2]{0:T(128)S(1)}, f32[2]{0:T(128)}, u32[]{:S(2)}) copy-start(f32[2]{0:T(128)} %param.11) | copy-start | bytes 28
  326.5 49.3 %copy-start.17 = (f32[2]{0:T(128)S(1)}, f32[2]{0:T(128)}, u32[]{:S(2)}) copy-start(f32[2]{0:T(128)} %integer_pow.13) | copy-start | bytes 28
  326.5 49.5 %copy-start.14 = (s32[512]{0:T(512)S(1)}, s32[512]{0:T(512)}, u32[]{:S(2)}) copy-start(s32[512]{0:T(512)} %param.14) | copy-start | bytes 6148
  326.5 53.9 %copy-start.1 = (f32[512]{0:T(512)S(1)}, f32[512]{0:T(512)}, u32[]{:S(2)}) copy-start(f32[512]{0:T(512)} %param.12) | copy-start | bytes 6148
Sparse Core Ops, SparseCore 0:
  225.3 26.1 all-gather.1
